TPU v7x, 32 devices: a whole 2x2x4 slice. The times are simulated.
32 devices in a mesh: gx: 4 (over z), gy: 4 (over y, x), gz: 2 (over core).
Axes of the slice: x: 2, y: 2, z: 4, core: 2. Of those that a mesh axis runs over, the one named last changes fastest.
Arguments:
- schur: bfloat16 [4, 4, 2, 2048, 2048], P('gx', 'gy', 'gz'), may hold values from -0.09375 to 0.09375
- interface_diag: float32 [4, 4, 2, 2048], P('gx', 'gy', 'gz'), may hold values from 2 to 4
- precond: float32 [4, 4, 2, 16, 128, 128], P('gx', 'gy', 'gz'), may hold values from -0.3 to 0.8
- load: bfloat16 [4, 4, 2, 2048, 256], P('gx', 'gy', 'gz'), may hold values from -170 to 170
- face_blocks: int32 [4, 4, 2, 6, 2], P('gx', 'gy', 'gz'), may hold values from 0 to 16, as said below
Outputs:
- solution: float32 [4, 4, 2, 2048, 256], P('gx', 'gy', 'gz')
- residual_norm: float32 [256], replicated
Inputs may be any that keep to these rules, and one draw needn't show every extreme that they name: `face_blocks`: for each subdomain p and direction d (0, 1: next and previous along the first grid dimension; 2, 3 and 4, 5 likewise along the second and third), slots 0 to n - 1 hold block numbers below 16 shared with the neighbour in that direction, where n (1 to 2 inside the grid, 0 across its boundary) equals the neighbour's n for the opposite direction, and the neighbour's slot k of the opposite direction holds the block that shares with p's slot k; the remaining slots hold 16; no block number appears twice in one subdomain's table; some face shares 2 blocks in every draw.
All inputs are finite; a program needn't handle non-finite values.
Results may differ from a plain program's by a relative error of at most 0.0008.
Values sent between devices are 32-bit elements; how exact they have to be, the bound alone decides.
A program may use at most 128 MiB of HBM per device.

v0:
```python
import jax
import jax.numpy as jnp
from jax import lax
from jax.sharding import PartitionSpec as P

epsilon = 1e-06


def extended_2(value, sides, width):
    for axis, dim in sides:
        peers, length = (lax.axis_size(axis), value.shape[dim])
        up = [(i, (i + 1) % peers) for i in range(peers - 1)]
        down = [(j, i) for i, j in up]
        last = lax.slice_in_dim(value, length - width, length, axis=dim)
        leading = lax.slice_in_dim(value, 0, width, axis=dim)
        before = lax.ppermute(last, axis, up)
        after = lax.ppermute(leading, axis, down)
        value = jnp.concatenate([before, value, after], axis=dim)
    return value


def assemble(blocks, slot_index, live_mask):
    block_count, block_rows, row_width = blocks.shape
    slot_count = slot_index.shape[1]
    extended = jnp.concatenate([blocks, jnp.zeros((1, block_rows, row_width), jnp.float32)], axis=0)
    slot_flat = slot_index.reshape(-1)
    packed = extended[slot_flat].reshape(6, slot_count, block_rows, row_width)
    gx_faces = extended_2(jnp.stack([packed[1], packed[0]], 0), (("gx", 0),), 1)
    gy_faces = extended_2(jnp.stack([packed[3], packed[2]], 0), (("gy", 0),), 1)
    gz_faces = extended_2(jnp.stack([packed[5], packed[4]], 0), (("gz", 0),), 1)
    arrived = jnp.stack(
        [gx_faces[3], gx_faces[0], gy_faces[3], gy_faces[0], gz_faces[3], gz_faces[0]], 0
    )
    extended = extended.at[slot_flat].add(arrived.reshape(6 * slot_count, block_rows, row_width))
    return extended[:block_count] * live_mask[:, None, None]


def partial_product(left_vec, right_vec):
    return 0.5 * jnp.sum(left_vec * right_vec, axis=(0, 1))


def on_device(schur, interface_diag, precond, load, face_blocks):
    block_count = precond.shape[3]
    block_rows = precond.shape[4]
    rhs_count = load.shape[-1]
    slot_index = face_blocks.reshape(6, face_blocks.shape[-1])
    slot_hits = slot_index[:, :, None] == jnp.arange(block_count, dtype=jnp.int32)
    live_mask = jnp.any(slot_hits, axis=(0, 1)).astype(jnp.float32)
    matrix = schur.reshape(schur.shape[-2], schur.shape[-1])
    diag_column = interface_diag.reshape(-1, 1)
    local_blocks = precond.reshape(block_count, block_rows, block_rows)
    assembled_load = assemble(
        load.reshape(block_count, block_rows, rhs_count).astype(jnp.float32), slot_index, live_mask
    )

    def precondition(vector):
        partial_value = jnp.einsum(
            "bij,bjr->bir", local_blocks, vector, precision=lax.Precision.HIGHEST
        )
        return assemble(partial_value, slot_index, live_mask)

    def operate(vector):
        flattened = vector.reshape(block_count * block_rows, rhs_count)
        narrow = flattened.astype(jnp.bfloat16)
        product = jnp.dot(matrix, narrow, preferred_element_type=jnp.float32)
        partial_value = product + diag_column * flattened
        return assemble(
            partial_value.reshape(block_count, block_rows, rhs_count), slot_index, live_mask
        )

    precond_raw = precondition(assembled_load)
    working_raw = operate(precond_raw)
    load_square, cross_first, raw_square = lax.psum(
        (
            partial_product(assembled_load, assembled_load),
            partial_product(working_raw, assembled_load),
            partial_product(working_raw, working_raw),
        ),
        ("gx", "gy", "gz"),
    )
    initial = jnp.sqrt(load_square + epsilon)
    rescale = 1.0 / initial
    basis_first = assembled_load * rescale
    precond_first = precond_raw * rescale
    diag_first = cross_first * rescale * rescale
    working = working_raw * rescale - diag_first * basis_first
    below_first = jnp.sqrt(
        jnp.maximum(raw_square * rescale * rescale - diag_first * diag_first, 0.0) + epsilon
    )
    basis_second = working / below_first
    precond_second = precondition(basis_second)
    working = operate(precond_second)
    upper_second, diag_second, work_square = lax.psum(
        (
            partial_product(working, basis_first),
            partial_product(working, basis_second),
            partial_product(working, working),
        ),
        ("gx", "gy", "gz"),
    )
    below_second = jnp.sqrt(
        jnp.maximum(work_square - upper_second * upper_second - diag_second * diag_second, 0.0)
        + epsilon
    )
    radius_first = jnp.sqrt(diag_first * diag_first + below_first * below_first)
    cosine_first = diag_first / radius_first
    sine_first = below_first / radius_first
    rotated_top = cosine_first * upper_second + sine_first * diag_second
    rotated_low = cosine_first * diag_second - sine_first * upper_second
    radius_second = jnp.sqrt(rotated_low * rotated_low + below_second * below_second)
    cosine_second = rotated_low / radius_second
    sine_second = below_second / radius_second
    weight_second = -initial * sine_first * cosine_second / radius_second
    weight_first = (initial * cosine_first - rotated_top * weight_second) / radius_first
    solution = weight_first * precond_first + weight_second * precond_second
    residual_norm = initial * sine_first * sine_second
    return (solution.reshape(1, 1, 1, block_count * block_rows, rhs_count), residual_norm)


def solution(mesh):
    placed = (
        P("gx", "gy", "gz", None, None),
        P("gx", "gy", "gz", None),
        P("gx", "gy", "gz", None, None, None),
        P("gx", "gy", "gz", None, None),
        P("gx", "gy", "gz", None, None),
    )
    return jax.shard_map(
        on_device,
        mesh=mesh,
        in_specs=placed,
        out_specs=(P("gx", "gy", "gz", None, None), P()),
        check_vma=False,
    )
```

profile of v0, /device:TPU:0, one launch (start us, length us, event | category | flops | bytes accessed | tf_op | source)
XLA Modules:
  0.0 332.9 jit_solution(5682009236857555295)
XLA Ops:
  7.7 5.6 %collective-permute-start.1 = (f32[1,2,128,256]{3,2,1,0:T(8,128)S(1)}, f32[1,2,128,256]{3,2,1,0:T(8,128)S(1)}, u32[]{:S(2)}, u32[]{:S(2)}) collective-permute-start(f32[1,2,128,256]{3,2,1,0:T(8,128)S(1)} %get-tuple-element.51), channel_id=1, source_target_pairs={{0,8},{8,16},{16,24},{1,9},{9,17},{17,25},{2,10},{10,18},{18,26},{... | collective-permute-start | bytes 786440 | tf_op jit(solution)/shard_map/ppermute | solution.py:16
  17.6 4.4 %collective-permute-start.3 = (f32[1,2,128,256]{3,2,1,0:T(8,128)S(1)}, f32[1,2,128,256]{3,2,1,0:T(8,128)S(1)}, u32[]{:S(2)}, u32[]{:S(2)}) collective-permute-start(f32[1,2,128,256]{3,2,1,0:T(8,128)S(1)} %get-tuple-element.49), channel_id=1, source_target_pairs={{0,2},{2,4},{4,6},{1,3},{3,5},{5,7},{8,10},{10,12},{12,14},{9,11},... | collective-permute-start | bytes 786440 | tf_op jit(solution)/shard_map/ppermute | solution.py:16
  22.1 4.8 %collective-permute-done.2 = f32[1,2,128,256]{3,2,1,0:T(8,128)S(1)} collective-permute-done((f32[1,2,128,256]{3,2,1,0:T(8,128)S(1)}, f32[1,2,128,256]{3,2,1,0:T(8,128)S(1)}, u32[]{:S(2)}, u32[]{:S(2)}) %collective-permute-start.2) | collective-permute-done | bytes 262176 | tf_op jit(solution)/shard_map/ppermute | solution.py:17
  33.0 3.8 %convolution_bitcast_fusion.1 = f32[16,128,256]{1,2,0:T(8,128)S(1)} fusion(f32[17,128,256]{2,1,0:T(8,128)S(1)} %scatter_fusion, f32[1,1,1,16,128,128]{5,4,3,2,1,0:T(8,128)S(1)} %copy-done, f32[16]{0:T(128)S(1)} %convert_element_type.24), kind=kOutput, calls=%fused_computation.32 | convolution fusion | flops 805830656 | bytes 5243392 | tf_op jit(solution)/shard_map/bij,bjr->bir/dot_general | solution.py:57
  38.5 3.4 %gather_fusion.1 = f32[12,128,256]{1,2,0:T(8,128)} fusion(f32[17,128,256]{1,2,0:T(8,128)} %concatenate.19, s32[1024]{0:T(1024)S(1)} %pad_clamp_fusion), kind=kCustom, calls=%fused_computation.1 | custom fusion | bytes 3145776 | tf_op jit(solution)/shard_map/gather | solution.py:27
  45.6 5.3 %collective-permute-start.7 = (f32[1,2,128,256]{2,3,1,0:T(8,128)}, f32[1,2,128,256]{2,3,1,0:T(8,128)}, u32[]{:S(2)}, u32[]{:S(2)}) collective-permute-start(f32[1,2,128,256]{2,3,1,0:T(8,128)} %get-tuple-element.45), channel_id=1, source_target_pairs={{0,8},{8,16},{16,24},{1,9},{9,17},{17,25},{2,10},{10,18},{18,26},{... | collective-permute-start | bytes 786440 | tf_op jit(solution)/shard_map/ppermute | solution.py:16
  58.0 6.6 %collective-permute-start.9 = (f32[1,2,128,256]{2,3,1,0:T(8,128)}, f32[1,2,128,256]{2,3,1,0:T(8,128)S(1)}, u32[]{:S(2)}, u32[]{:S(2)}) collective-permute-start(f32[1,2,128,256]{2,3,1,0:T(8,128)} %get-tuple-element.43), channel_id=1, source_target_pairs={{0,2},{2,4},{4,6},{1,3},{3,5},{5,7},{8,10},{10,12},{12,14},{9,11},... | collective-permute-start | bytes 786440 | tf_op jit(solution)/shard_map/ppermute | solution.py:16
  76.3 4.5 %scatter_fusion.1 = f32[17,128,256]{2,1,0:T(8,128)} fusion(f32[17,128,256]{2,1,0:T(8,128)} %copy.23, s32[12]{0:T(128)S(1)} %fusion.24, f32[12,128,256]{2,1,0:T(8,128)} %copy.24), kind=kCustom, calls=%fused_computation.6 | custom fusion | flops 393216 | bytes 4718640 | tf_op jit(solution)/shard_map/scatter-add | solution.py:34
  80.8 3.6 %fusion.28 = (bf16[16,128,256]{2,1,0:T(8,128)(2,1)}, f32[16,128,256]{2,1,0:T(8,128)}) fusion(f32[16]{0:T(128)S(1)} %convert_element_type.24, f32[17,128,256]{2,1,0:T(8,128)} %scatter_fusion.1), kind=kLoop, calls=%fused_computation.126 | loop fusion | flops 1048576 | bytes 5242944 | tf_op jit(solution)/shard_map/convert_element_type | solution.py:64
  87.4 8.0 %fusion.13 = f32[2048,256]{0,1:T(8,128)} fusion(bf16[2048,256]{1,0:T(8,128)(2,1)} %bitcast.116, bf16[1,1,1,2048,2048]{4,3,2,1,0:T(8,128)(2,1)} %param.5, f32[2048,256]{0,1:T(8,128)} %copy.25, f32[2048]{0:T(1024)S(1)} %bitcast.119), kind=kOutput, calls=%fused_computation.17 | convolution fusion | flops 2148532224 | bytes 13639680 | tf_op jit(solution)/shard_map/dot_general | solution.py:65
  101.4 3.4 %gather_fusion.2 = f32[12,128,256]{2,1,0:T(8,128)} fusion(f32[17,128,256]{2,1,0:T(8,128)} %concatenate.20, s32[1024]{0:T(1024)S(1)} %pad_clamp_fusion), kind=kCustom, calls=%fused_computation.2 | custom fusion | bytes 3145776 | tf_op jit(solution)/shard_map/gather | solution.py:27
  107.7 4.6 %collective-permute-start.13 = (f32[1,2,128,256]{3,2,1,0:T(8,128)S(1)}, f32[1,2,128,256]{3,2,1,0:T(8,128)S(1)}, u32[]{:S(2)}, u32[]{:S(2)}) collective-permute-start(f32[1,2,128,256]{3,2,1,0:T(8,128)S(1)} %get-tuple-element.39), channel_id=1, source_target_pairs={{0,8},{8,16},{16,24},{1,9},{9,17},{17,25},{2,10},{10,18},{18,26},{... | collective-permute-start | bytes 786440 | tf_op jit(solution)/shard_map/ppermute | solution.py:16
  116.8 5.6 %collective-permute-start.15 = (f32[1,2,128,256]{3,2,1,0:T(8,128)S(1)}, f32[1,2,128,256]{3,2,1,0:T(8,128)S(1)}, u32[]{:S(2)}, u32[]{:S(2)}) collective-permute-start(f32[1,2,128,256]{3,2,1,0:T(8,128)S(1)} %get-tuple-element.37), channel_id=1, source_target_pairs={{0,2},{2,4},{4,6},{1,3},{3,5},{5,7},{8,10},{10,12},{12,14},{9,11},... | collective-permute-start | bytes 786440 | tf_op jit(solution)/shard_map/ppermute | solution.py:16
  124.5 4.3 %collective-permute-done.15 = f32[1,2,128,256]{3,2,1,0:T(8,128)S(1)} collective-permute-done((f32[1,2,128,256]{3,2,1,0:T(8,128)S(1)}, f32[1,2,128,256]{3,2,1,0:T(8,128)S(1)}, u32[]{:S(2)}, u32[]{:S(2)}) %collective-permute-start.15) | collective-permute-done | bytes 262176 | tf_op jit(solution)/shard_map/ppermute | solution.py:16
  131.1 4.7 %scatter_fusion.2 = f32[17,128,256]{2,1,0:T(8,128)} fusion(f32[17,128,256]{2,1,0:T(8,128)} %concatenate.20, s32[12]{0:T(128)S(1)} %fusion.24, f32[12,128,256]{2,1,0:T(8,128)} %bitcast.31), kind=kCustom, calls=%fused_computation.7 | custom fusion | flops 393216 | bytes 4718640 | tf_op jit(solution)/shard_map/scatter-add | solution.py:34
  138.0 43.7 %all-reduce.6 = (f32[256]{0:T(256)S(1)}, f32[256]{0:T(256)S(1)}, f32[256]{0:T(256)S(1)}) all-reduce(f32[256]{0:T(256)S(1)} %broadcast_multiply_fusion.5, f32[256]{0:T(256)S(1)} %get-tuple-element.54, f32[256]{0:T(256)S(1)} %get-tuple-element.55), channel_id=1, replica_groups=mesh['gx'=4,'gy'=4,'gz'=2] {'gx','gy','gz'}, use_global_device_ids=true, to_apply=%region_3.0 | all-reduce | flops 768 | bytes 6144 | tf_op jit(solution)/shard_map/psum | solution.py:73
  181.7 5.7 %convolution_bitcast_fusion = f32[16,128,256]{1,2,0:T(8,128)S(1)} fusion(f32[1,1,1,16,128,128]{5,4,3,2,1,0:T(8,128)S(1)} %copy-done, f32[17,128,256]{2,1,0:T(8,128)} %scatter_fusion.2, f32[17,128,256]{2,1,0:T(8,128)S(1)} %scatter_fusion, f32[256]{0:T(256)S(1)} %get-tuple-element.18, f32[256]{0:T(256)S(1)} %get-tuple-element.19, ...), kind=kOutput, calls=%fused_computation.31 | convolution fusion | flops 808976384 | bytes 7343616 | tf_op jit(solution)/shard_map/bij,bjr->bir/dot_general | solution.py:57
  189.1 3.4 %gather_fusion.3 = f32[12,128,256]{1,2,0:T(8,128)} fusion(f32[17,128,256]{1,2,0:T(8,128)} %concatenate.21, s32[1024]{0:T(1024)S(1)} %pad_clamp_fusion), kind=kCustom, calls=%fused_computation.3 | custom fusion | bytes 3145776 | tf_op jit(solution)/shard_map/gather | solution.py:27
  195.9 5.3 %collective-permute-start.19 = (f32[1,2,128,256]{2,3,1,0:T(8,128)S(1)}, f32[1,2,128,256]{2,3,1,0:T(8,128)}, u32[]{:S(2)}, u32[]{:S(2)}) collective-permute-start(f32[1,2,128,256]{2,3,1,0:T(8,128)S(1)} %get-tuple-element.33), channel_id=1, source_target_pairs={{0,8},{8,16},{16,24},{1,9},{9,17},{17,25},{2,10},{10,18},{18,26},{... | collective-permute-start | bytes 786440 | tf_op jit(solution)/shard_map/ppermute | solution.py:16
  208.1 4.8 %collective-permute-start.21 = (f32[1,2,128,256]{2,3,1,0:T(8,128)S(1)}, f32[1,2,128,256]{2,3,1,0:T(8,128)S(1)}, u32[]{:S(2)}, u32[]{:S(2)}) collective-permute-start(f32[1,2,128,256]{2,3,1,0:T(8,128)S(1)} %get-tuple-element.31), channel_id=1, source_target_pairs={{0,2},{2,4},{4,6},{1,3},{3,5},{5,7},{8,10},{10,12},{12,14},{9,11},... | collective-permute-start | bytes 786440 | tf_op jit(solution)/shard_map/ppermute | solution.py:16
  224.7 4.5 %scatter_fusion.3 = f32[17,128,256]{2,1,0:T(8,128)} fusion(f32[17,128,256]{2,1,0:T(8,128)} %copy.28, s32[12]{0:T(128)S(1)} %fusion.24, f32[12,128,256]{2,1,0:T(8,128)} %copy.29), kind=kCustom, calls=%fused_computation.8 | custom fusion | flops 393216 | bytes 4718640 | tf_op jit(solution)/shard_map/scatter-add | solution.py:34
  229.2 3.3 fusion.27
  235.4 7.7 %fusion.10 = f32[2048,256]{0,1:T(8,128)} fusion(bf16[2048,256]{1,0:T(8,128)(2,1)S(1)} %bitcast.117, bf16[1,1,1,2048,2048]{4,3,2,1,0:T(8,128)(2,1)} %param.5, f32[2048,256]{0,1:T(8,128)} %copy.30, f32[2048]{0:T(1024)S(1)} %bitcast.120), kind=kOutput, calls=%fused_computation.16 | convolution fusion | flops 2148532224 | bytes 13639680 | tf_op jit(solution)/shard_map/dot_general | solution.py:65
  246.1 3.2 concatenate.22
  249.3 3.4 %gather_fusion.4 = f32[12,128,256]{2,1,0:T(8,128)} fusion(f32[17,128,256]{2,1,0:T(8,128)} %concatenate.22, s32[1024]{0:T(1024)S(1)} %pad_clamp_fusion), kind=kCustom, calls=%fused_computation.4 | custom fusion | bytes 3145776 | tf_op jit(solution)/shard_map/gather | solution.py:27
  255.5 4.6 %collective-permute-start.25 = (f32[1,2,128,256]{3,2,1,0:T(8,128)S(1)}, f32[1,2,128,256]{3,2,1,0:T(8,128)S(1)}, u32[]{:S(2)}, u32[]{:S(2)}) collective-permute-start(f32[1,2,128,256]{3,2,1,0:T(8,128)S(1)} %get-tuple-element.27), channel_id=1, source_target_pairs={{0,8},{8,16},{16,24},{1,9},{9,17},{17,25},{2,10},{10,18},{18,26},{... | collective-permute-start | bytes 786440 | tf_op jit(solution)/shard_map/ppermute | solution.py:16
  264.6 5.5 %collective-permute-start.27 = (f32[1,2,128,256]{3,2,1,0:T(8,128)S(1)}, f32[1,2,128,256]{3,2,1,0:T(8,128)S(1)}, u32[]{:S(2)}, u32[]{:S(2)}) collective-permute-start(f32[1,2,128,256]{3,2,1,0:T(8,128)S(1)} %get-tuple-element.25), channel_id=1, source_target_pairs={{0,2},{2,4},{4,6},{1,3},{3,5},{5,7},{8,10},{10,12},{12,14},{9,11},... | collective-permute-start | bytes 786440 | tf_op jit(solution)/shard_map/ppermute | solution.py:16
  272.3 4.0 %collective-permute-done.27 = f32[1,2,128,256]{3,2,1,0:T(8,128)S(1)} collective-permute-done((f32[1,2,128,256]{3,2,1,0:T(8,128)S(1)}, f32[1,2,128,256]{3,2,1,0:T(8,128)S(1)}, u32[]{:S(2)}, u32[]{:S(2)}) %collective-permute-start.27) | collective-permute-done | bytes 262176 | tf_op jit(solution)/shard_map/ppermute | solution.py:16
  278.6 4.5 %scatter_fusion.4 = f32[17,128,256]{2,1,0:T(8,128)} fusion(f32[17,128,256]{2,1,0:T(8,128)} %concatenate.22, s32[12]{0:T(128)S(1)} %fusion.24, f32[12,128,256]{2,1,0:T(8,128)} %bitcast.50), kind=kCustom, calls=%fused_computation.9 | custom fusion | flops 393216 | bytes 4718640 | tf_op jit(solution)/shard_map/scatter-add | solution.py:34
  283.0 3.2 multiply_reduce_fusion.2
  286.3 42.0 %all-reduce.5 = (f32[256]{0:T(256)S(1)}, f32[256]{0:T(256)S(1)}, f32[256]{0:T(256)S(1)}) all-reduce(f32[256]{0:T(256)S(1)} %broadcast_multiply_fusion.1, f32[256]{0:T(256)S(1)} %broadcast_multiply_fusion, f32[256]{0:T(256)S(1)} %broadcast_multiply_fusion.2), channel_id=1, replica_groups=mesh['gx'=4,'gy'=4,'gz'=2] {'gx','gy','gz'}, use_global_device_ids=true, to_apply=%region_15.0 | all-reduce | flops 768 | bytes 6144 | tf_op jit(solution)/shard_map/psum | solution.py:93
  328.9 4.0 %multiply_add_fusion = f32[16,128,256]{2,1,0:T(8,128)} fusion(f32[16,128,256]{2,1,0:T(8,128)} %get-tuple-element.17, f32[16,128,256]{2,1,0:T(8,128)} %get-tuple-element.22, f32[256]{0:T(256)S(1)} %get-tuple-element.15, f32[256]{0:T(256)S(1)} %get-tuple-element.14, f32[256]{0:T(256)S(1)} %get-tuple-element.20), kind=kLoop, calls=%fused_computation.23 | loop fusion | flops 2097152 | bytes 6294528 | tf_op jit(solution)/shard_map/add | solution.py:115
  (134 shorter events, 106.4 us)
Async XLA Ops:
  0.6 32.4 %copy-start = (f32[1,1,1,16,128,128]{5,4,3,2,1,0:T(8,128)S(1)}, f32[1,1,1,16,128,128]{5,4,3,2,1,0:T(8,128)}, u32[]{:S(2)}) copy-start(f32[1,1,1,16,128,128]{5,4,3,2,1,0:T(8,128)} %param.7) | copy-start | bytes 3145732
  6.4 11.3 %collective-permute-start = (f32[1,2,128,256]{3,2,1,0:T(8,128)S(1)}, f32[1,2,128,256]{3,2,1,0:T(8,128)S(1)}, u32[]{:S(2)}, u32[]{:S(2)}) collective-permute-start(f32[1,2,128,256]{3,2,1,0:T(8,128)S(1)} %get-tuple-element.52), channel_id=1, source_target_pairs={{8,0},{16,8},{24,16},{9,1},{17,9},{25,17},{10,2},{18,10},{26,18},{... | collective-permute-start | bytes 786440 | tf_op jit(solution)/shard_map/ppermute | solution.py:17
  7.7 14.4 %collective-permute-start.1 = (f32[1,2,128,256]{3,2,1,0:T(8,128)S(1)}, f32[1,2,128,256]{3,2,1,0:T(8,128)S(1)}, u32[]{:S(2)}, u32[]{:S(2)}) collective-permute-start(f32[1,2,128,256]{3,2,1,0:T(8,128)S(1)} %get-tuple-element.51), channel_id=1, source_target_pairs={{0,8},{8,16},{16,24},{1,9},{9,17},{17,25},{2,10},{10,18},{18,26},{... | collective-permute-start | bytes 786440 | tf_op jit(solution)/shard_map/ppermute | solution.py:16
  13.3 15.4 %collective-permute-start.5 = (f32[1,2,128,256]{3,2,1,0:T(8,128)S(1)}, f32[1,2,128,256]{3,2,1,0:T(8,128)S(1)}, u32[]{:S(2)}, u32[]{:S(2)}) collective-permute-start(f32[1,2,128,256]{3,2,1,0:T(8,128)S(1)} %get-tuple-element.47), channel_id=1, source_target_pairs={{0,1},{2,3},{4,5},{6,7},{8,9},{10,11},{12,13},{14,15},{16,17},{18,... | collective-permute-start | bytes 786440 | tf_op jit(solution)/shard_map/ppermute | solution.py:16
  14.8 13.9 %collective-permute-start.4 = (f32[1,2,128,256]{3,2,1,0:T(8,128)S(1)}, f32[1,2,128,256]{3,2,1,0:T(8,128)S(1)}, u32[]{:S(2)}, u32[]{:S(2)}) collective-permute-start(f32[1,2,128,256]{3,2,1,0:T(8,128)S(1)} %get-tuple-element.48), channel_id=1, source_target_pairs={{1,0},{3,2},{5,4},{7,6},{9,8},{11,10},{13,12},{15,14},{17,16},{19,... | collective-permute-start | bytes 786440 | tf_op jit(solution)/shard_map/ppermute | solution.py:17
  16.1 10.9 %collective-permute-start.2 = (f32[1,2,128,256]{3,2,1,0:T(8,128)S(1)}, f32[1,2,128,256]{3,2,1,0:T(8,128)S(1)}, u32[]{:S(2)}, u32[]{:S(2)}) collective-permute-start(f32[1,2,128,256]{3,2,1,0:T(8,128)S(1)} %get-tuple-element.50), channel_id=1, source_target_pairs={{2,0},{4,2},{6,4},{3,1},{5,3},{7,5},{10,8},{12,10},{14,12},{11,9},... | collective-permute-start | bytes 786440 | tf_op jit(solution)/shard_map/ppermute | solution.py:17
  17.6 11.0 %collective-permute-start.3 = (f32[1,2,128,256]{3,2,1,0:T(8,128)S(1)}, f32[1,2,128,256]{3,2,1,0:T(8,128)S(1)}, u32[]{:S(2)}, u32[]{:S(2)}) collective-permute-start(f32[1,2,128,256]{3,2,1,0:T(8,128)S(1)} %get-tuple-element.49), channel_id=1, source_target_pairs={{0,2},{2,4},{4,6},{1,3},{3,5},{5,7},{8,10},{10,12},{12,14},{9,11},... | collective-permute-start | bytes 786440 | tf_op jit(solution)/shard_map/ppermute | solution.py:16
  44.3 13.6 %collective-permute-start.6 = (f32[1,2,128,256]{2,3,1,0:T(8,128)}, f32[1,2,128,256]{2,3,1,0:T(8,128)}, u32[]{:S(2)}, u32[]{:S(2)}) collective-permute-start(f32[1,2,128,256]{2,3,1,0:T(8,128)} %get-tuple-element.46), channel_id=1, source_target_pairs={{8,0},{16,8},{24,16},{9,1},{17,9},{25,17},{10,2},{18,10},{26,18},{... | collective-permute-start | bytes 786440 | tf_op jit(solution)/shard_map/ppermute | solution.py:17
  45.6 20.6 %collective-permute-start.7 = (f32[1,2,128,256]{2,3,1,0:T(8,128)}, f32[1,2,128,256]{2,3,1,0:T(8,128)}, u32[]{:S(2)}, u32[]{:S(2)}) collective-permute-start(f32[1,2,128,256]{2,3,1,0:T(8,128)} %get-tuple-element.45), channel_id=1, source_target_pairs={{0,8},{8,16},{16,24},{1,9},{9,17},{17,25},{2,10},{10,18},{18,26},{... | collective-permute-start | bytes 786440 | tf_op jit(solution)/shard_map/ppermute | solution.py:16
  50.9 17.0 %collective-permute-start.8 = (f32[1,2,128,256]{2,3,1,0:T(8,128)}, f32[1,2,128,256]{2,3,1,0:T(8,128)}, u32[]{:S(2)}, u32[]{:S(2)}) collective-permute-start(f32[1,2,128,256]{2,3,1,0:T(8,128)} %get-tuple-element.44), channel_id=1, source_target_pairs={{2,0},{4,2},{6,4},{3,1},{5,3},{7,5},{10,8},{12,10},{14,12},{11,9},... | collective-permute-start | bytes 786440 | tf_op jit(solution)/shard_map/ppermute | solution.py:17
  55.2 17.4 %collective-permute-start.11 = (f32[1,2,128,256]{2,3,1,0:T(8,128)S(1)}, f32[1,2,128,256]{2,3,1,0:T(8,128)S(1)}, u32[]{:S(2)}, u32[]{:S(2)}) collective-permute-start(f32[1,2,128,256]{2,3,1,0:T(8,128)S(1)} %get-tuple-element.41), channel_id=1, source_target_pairs={{0,1},{2,3},{4,5},{6,7},{8,9},{10,11},{12,13},{14,15},{16,17},{18,... | collective-permute-start | bytes 786440 | tf_op jit(solution)/shard_map/ppermute | solution.py:16
  56.6 15.2 %collective-permute-start.10 = (f32[1,2,128,256]{2,3,1,0:T(8,128)}, f32[1,2,128,256]{2,3,1,0:T(8,128)S(1)}, u32[]{:S(2)}, u32[]{:S(2)}) collective-permute-start(f32[1,2,128,256]{2,3,1,0:T(8,128)} %get-tuple-element.42), channel_id=1, source_target_pairs={{1,0},{3,2},{5,4},{7,6},{9,8},{11,10},{13,12},{15,14},{17,16},{19,... | collective-permute-start | bytes 786440 | tf_op jit(solution)/shard_map/ppermute | solution.py:17
  58.0 13.2 %collective-permute-start.9 = (f32[1,2,128,256]{2,3,1,0:T(8,128)}, f32[1,2,128,256]{2,3,1,0:T(8,128)S(1)}, u32[]{:S(2)}, u32[]{:S(2)}) collective-permute-start(f32[1,2,128,256]{2,3,1,0:T(8,128)} %get-tuple-element.43), channel_id=1, source_target_pairs={{0,2},{2,4},{4,6},{1,3},{3,5},{5,7},{8,10},{10,12},{12,14},{9,11},... | collective-permute-start | bytes 786440 | tf_op jit(solution)/shard_map/ppermute | solution.py:16
  106.4 10.4 %collective-permute-start.12 = (f32[1,2,128,256]{3,2,1,0:T(8,128)S(1)}, f32[1,2,128,256]{3,2,1,0:T(8,128)S(1)}, u32[]{:S(2)}, u32[]{:S(2)}) collective-permute-start(f32[1,2,128,256]{3,2,1,0:T(8,128)S(1)} %get-tuple-element.40), channel_id=1, source_target_pairs={{8,0},{16,8},{24,16},{9,1},{17,9},{25,17},{10,2},{18,10},{26,18},{... | collective-permute-start | bytes 786440 | tf_op jit(solution)/shard_map/ppermute | solution.py:17
  107.7 15.4 %collective-permute-start.13 = (f32[1,2,128,256]{3,2,1,0:T(8,128)S(1)}, f32[1,2,128,256]{3,2,1,0:T(8,128)S(1)}, u32[]{:S(2)}, u32[]{:S(2)}) collective-permute-start(f32[1,2,128,256]{3,2,1,0:T(8,128)S(1)} %get-tuple-element.39), channel_id=1, source_target_pairs={{0,8},{8,16},{16,24},{1,9},{9,17},{17,25},{2,10},{10,18},{18,26},{... | collective-permute-start | bytes 786440 | tf_op jit(solution)/shard_map/ppermute | solution.py:16
  112.3 11.5 %collective-permute-start.14 = (f32[1,2,128,256]{3,2,1,0:T(8,128)S(1)}, f32[1,2,128,256]{3,2,1,0:T(8,128)S(1)}, u32[]{:S(2)}, u32[]{:S(2)}) collective-permute-start(f32[1,2,128,256]{3,2,1,0:T(8,128)S(1)} %get-tuple-element.38), channel_id=1, source_target_pairs={{2,0},{4,2},{6,4},{3,1},{5,3},{7,5},{10,8},{12,10},{14,12},{11,9},... | collective-permute-start | bytes 786440 | tf_op jit(solution)/shard_map/ppermute | solution.py:17
  113.6 16.8 %collective-permute-start.17 = (f32[1,2,128,256]{3,2,1,0:T(8,128)S(1)}, f32[1,2,128,256]{3,2,1,0:T(8,128)S(1)}, u32[]{:S(2)}, u32[]{:S(2)}) collective-permute-start(f32[1,2,128,256]{3,2,1,0:T(8,128)S(1)} %get-tuple-element.35), channel_id=1, source_target_pairs={{0,1},{2,3},{4,5},{6,7},{8,9},{10,11},{12,13},{14,15},{16,17},{18,... | collective-permute-start | bytes 786440 | tf_op jit(solution)/shard_map/ppermute | solution.py:16
  115.2 14.4 %collective-permute-start.16 = (f32[1,2,128,256]{3,2,1,0:T(8,128)S(1)}, f32[1,2,128,256]{3,2,1,0:T(8,128)S(1)}, u32[]{:S(2)}, u32[]{:S(2)}) collective-permute-start(f32[1,2,128,256]{3,2,1,0:T(8,128)S(1)} %get-tuple-element.36), channel_id=1, source_target_pairs={{1,0},{3,2},{5,4},{7,6},{9,8},{11,10},{13,12},{15,14},{17,16},{19,... | collective-permute-start | bytes 786440 | tf_op jit(solution)/shard_map/ppermute | solution.py:17
  116.8 12.1 %collective-permute-start.15 = (f32[1,2,128,256]{3,2,1,0:T(8,128)S(1)}, f32[1,2,128,256]{3,2,1,0:T(8,128)S(1)}, u32[]{:S(2)}, u32[]{:S(2)}) collective-permute-start(f32[1,2,128,256]{3,2,1,0:T(8,128)S(1)} %get-tuple-element.37), channel_id=1, source_target_pairs={{0,2},{2,4},{4,6},{1,3},{3,5},{5,7},{8,10},{10,12},{12,14},{9,11},... | collective-permute-start | bytes 786440 | tf_op jit(solution)/shard_map/ppermute | solution.py:16
  194.7 13.5 %collective-permute-start.18 = (f32[1,2,128,256]{2,3,1,0:T(8,128)}, f32[1,2,128,256]{2,3,1,0:T(8,128)}, u32[]{:S(2)}, u32[]{:S(2)}) collective-permute-start(f32[1,2,128,256]{2,3,1,0:T(8,128)} %get-tuple-element.34), channel_id=1, source_target_pairs={{8,0},{16,8},{24,16},{9,1},{17,9},{25,17},{10,2},{18,10},{26,18},{... | collective-permute-start | bytes 786440 | tf_op jit(solution)/shard_map/ppermute | solution.py:17
  195.9 18.7 %collective-permute-start.19 = (f32[1,2,128,256]{2,3,1,0:T(8,128)S(1)}, f32[1,2,128,256]{2,3,1,0:T(8,128)}, u32[]{:S(2)}, u32[]{:S(2)}) collective-permute-start(f32[1,2,128,256]{2,3,1,0:T(8,128)S(1)} %get-tuple-element.33), channel_id=1, source_target_pairs={{0,8},{8,16},{16,24},{1,9},{9,17},{17,25},{2,10},{10,18},{18,26},{... | collective-permute-start | bytes 786440 | tf_op jit(solution)/shard_map/ppermute | solution.py:16
  201.2 15.1 %collective-permute-start.20 = (f32[1,2,128,256]{2,3,1,0:T(8,128)S(1)}, f32[1,2,128,256]{2,3,1,0:T(8,128)}, u32[]{:S(2)}, u32[]{:S(2)}) collective-permute-start(f32[1,2,128,256]{2,3,1,0:T(8,128)S(1)} %get-tuple-element.32), channel_id=1, source_target_pairs={{2,0},{4,2},{6,4},{3,1},{5,3},{7,5},{10,8},{12,10},{14,12},{11,9},... | collective-permute-start | bytes 786440 | tf_op jit(solution)/shard_map/ppermute | solution.py:17
  205.5 15.4 %collective-permute-start.23 = (f32[1,2,128,256]{2,3,1,0:T(8,128)S(1)}, f32[1,2,128,256]{2,3,1,0:T(8,128)S(1)}, u32[]{:S(2)}, u32[]{:S(2)}) collective-permute-start(f32[1,2,128,256]{2,3,1,0:T(8,128)S(1)} %get-tuple-element.29), channel_id=1, source_target_pairs={{0,1},{2,3},{4,5},{6,7},{8,9},{10,11},{12,13},{14,15},{16,17},{18,... | collective-permute-start | bytes 786440 | tf_op jit(solution)/shard_map/ppermute | solution.py:16
  206.8 13.4 %collective-permute-start.22 = (f32[1,2,128,256]{2,3,1,0:T(8,128)S(1)}, f32[1,2,128,256]{2,3,1,0:T(8,128)S(1)}, u32[]{:S(2)}, u32[]{:S(2)}) collective-permute-start(f32[1,2,128,256]{2,3,1,0:T(8,128)S(1)} %get-tuple-element.30), channel_id=1, source_target_pairs={{1,0},{3,2},{5,4},{7,6},{9,8},{11,10},{13,12},{15,14},{17,16},{19,... | collective-permute-start | bytes 786440 | tf_op jit(solution)/shard_map/ppermute | solution.py:17
  208.1 11.3 %collective-permute-start.21 = (f32[1,2,128,256]{2,3,1,0:T(8,128)S(1)}, f32[1,2,128,256]{2,3,1,0:T(8,128)S(1)}, u32[]{:S(2)}, u32[]{:S(2)}) collective-permute-start(f32[1,2,128,256]{2,3,1,0:T(8,128)S(1)} %get-tuple-element.31), channel_id=1, source_target_pairs={{0,2},{2,4},{4,6},{1,3},{3,5},{5,7},{8,10},{10,12},{12,14},{9,11},... | collective-permute-start | bytes 786440 | tf_op jit(solution)/shard_map/ppermute | solution.py:16
  254.2 10.4 %collective-permute-start.24 = (f32[1,2,128,256]{3,2,1,0:T(8,128)S(1)}, f32[1,2,128,256]{3,2,1,0:T(8,128)S(1)}, u32[]{:S(2)}, u32[]{:S(2)}) collective-permute-start(f32[1,2,128,256]{3,2,1,0:T(8,128)S(1)} %get-tuple-element.28), channel_id=1, source_target_pairs={{8,0},{16,8},{24,16},{9,1},{17,9},{25,17},{10,2},{18,10},{26,18},{... | collective-permute-start | bytes 786440 | tf_op jit(solution)/shard_map/ppermute | solution.py:17
  255.5 15.3 %collective-permute-start.25 = (f32[1,2,128,256]{3,2,1,0:T(8,128)S(1)}, f32[1,2,128,256]{3,2,1,0:T(8,128)S(1)}, u32[]{:S(2)}, u32[]{:S(2)}) collective-permute-start(f32[1,2,128,256]{3,2,1,0:T(8,128)S(1)} %get-tuple-element.27), channel_id=1, source_target_pairs={{0,8},{8,16},{16,24},{1,9},{9,17},{17,25},{2,10},{10,18},{18,26},{... | collective-permute-start | bytes 786440 | tf_op jit(solution)/shard_map/ppermute | solution.py:16
  260.1 11.5 %collective-permute-start.26 = (f32[1,2,128,256]{3,2,1,0:T(8,128)S(1)}, f32[1,2,128,256]{3,2,1,0:T(8,128)S(1)}, u32[]{:S(2)}, u32[]{:S(2)}) collective-permute-start(f32[1,2,128,256]{3,2,1,0:T(8,128)S(1)} %get-tuple-element.26), channel_id=1, source_target_pairs={{2,0},{4,2},{6,4},{3,1},{5,3},{7,5},{10,8},{12,10},{14,12},{11,9},... | collective-permute-start | bytes 786440 | tf_op jit(solution)/shard_map/ppermute | solution.py:17
  261.4 16.4 %collective-permute-start.29 = (f32[1,2,128,256]{3,2,1,0:T(8,128)S(1)}, f32[1,2,128,256]{3,2,1,0:T(8,128)S(1)}, u32[]{:S(2)}, u32[]{:S(2)}) collective-permute-start(f32[1,2,128,256]{3,2,1,0:T(8,128)S(1)} %get-tuple-element.23), channel_id=1, source_target_pairs={{0,1},{2,3},{4,5},{6,7},{8,9},{10,11},{12,13},{14,15},{16,17},{18,... | collective-permute-start | bytes 786440 | tf_op jit(solution)/shard_map/ppermute | solution.py:16
  263.0 14.1 %collective-permute-start.28 = (f32[1,2,128,256]{3,2,1,0:T(8,128)S(1)}, f32[1,2,128,256]{3,2,1,0:T(8,128)S(1)}, u32[]{:S(2)}, u32[]{:S(2)}) collective-permute-start(f32[1,2,128,256]{3,2,1,0:T(8,128)S(1)} %get-tuple-element.24), channel_id=1, source_target_pairs={{1,0},{3,2},{5,4},{7,6},{9,8},{11,10},{13,12},{15,14},{17,16},{19,... | collective-permute-start | bytes 786440 | tf_op jit(solution)/shard_map/ppermute | solution.py:17
  264.6 11.8 %collective-permute-start.27 = (f32[1,2,128,256]{3,2,1,0:T(8,128)S(1)}, f32[1,2,128,256]{3,2,1,0:T(8,128)S(1)}, u32[]{:S(2)}, u32[]{:S(2)}) collective-permute-start(f32[1,2,128,256]{3,2,1,0:T(8,128)S(1)} %get-tuple-element.25), channel_id=1, source_target_pairs={{0,2},{2,4},{4,6},{1,3},{3,5},{5,7},{8,10},{10,12},{12,14},{9,11},... | collective-permute-start | bytes 786440 | tf_op jit(solution)/shard_map/ppermute | solution.py:16
  283.0 45.3 %copy-start.8 = (f32[256]{0:T(256)S(1)}, f32[256]{0:T(256)}, u32[]{:S(2)}) copy-start(f32[256]{0:T(256)} %copy-done.7) | copy-start | bytes 3076
  (10 other events, 49.6 us)
where the time goes:
time: 335 us; the launch traced here: 333 us
  blocking collectives  85.7 us (26%)
  local copies, waits for them, and re-layouts  83.5 us (25%)
  starting transfers between devices  78.9 us (24%)
  other arithmetic  39.8 us (12%)
  matrix products  25.2 us (8%)
  waiting for transfers between devices  18.6 us (6%)
    ppermute x15, starting transfers between devices, extended_2(): before = lax.ppermute(last, axis, up)  59.6 us
    psum x1, blocking collectives, on_device(): lax.psum((partial_product(assembled_load, assembled_load), partial_produc...  43.7 us
    psum x1, blocking collectives, on_device(): lax.psum((partial_product(working, basis_first), partial_product(working,...  42 us
    unnamed x50, local copies, waits for them, and re-layouts  22.4 us
    scatter-add x5, other arithmetic, assemble(): extended.at[slot_flat]  21.2 us
    ppermute x15, starting transfers between devices, extended_2(): after = lax.ppermute(leading, axis, down)  19.3 us
    dot_general x2, matrix products, operate(): product = jnp.dot(matrix, narrow, preferred_element_type=jnp.float32)  15.7 us
    concatenate x6, local copies, waits for them, and re-layouts, assemble(): jnp.concatenate([blocks, jnp.zeros((1, block_rows, row_width), jnp.float3...  15.7 us
  transfers between devices with their start and end apart: 30, of which 9 were waited for; matrix products, arithmetic and copies ran while one was open for 8% of the time, Pallas kernels for 0%

commit v1 on v0

v1 whole, which is shorter than its diff:
```python
import functools

import jax
import jax.numpy as jnp
from jax import lax
from jax.experimental import pallas as pl
from jax.experimental.pallas import tpu as pltpu
from jax.sharding import PartitionSpec as P

EPS = 1e-06
MESH = pl.DeviceIdType.MESH
AXES = ("gx", "gy", "gz")
LANES = 128
F32 = jnp.float32
BF16 = jnp.bfloat16


def kernel(
    sizes,
    load_send,
    prec_send,
    schur_slots,
    diag_slots,
    mask_ref,
    out_ref,
    norm_ref,
    load_recv,
    prec_recv,
    prec_split,
    rhs,
    z1_ref,
    z2_ref,
    z_narrow,
    u1_send,
    u1_recv,
    q_ref,
    u2_send,
    u2_recv,
    plane_buf,
    line_buf,
    face_send,
    face_recv,
    plane_send,
    plane_recv,
    line_send,
    line_recv,
):
    nx, ny, nz = sizes
    planes = ny * nz
    cap, blk = prec_send.shape[1:3]
    cols = load_send.shape[-1]
    slots = 6 * cap
    rows = cap * blk
    gx, gy, gz = (lax.axis_index(a) for a in AXES)
    here = gy * nz + gz

    def plane_peer(step):
        other = lax.rem(here + step, planes)
        return (gx, other // nz, lax.rem(other, nz))

    def line_peer(step):
        return (lax.rem(gx + step, nx), gy, gz)

    barrier = pltpu.get_barrier_semaphore()
    for step in range(1, planes):
        pl.semaphore_signal(barrier, inc=1, device_id=plane_peer(step), device_id_type=MESH)
    for step in range(1, nx):
        pl.semaphore_signal(barrier, inc=1, device_id=line_peer(step), device_id_type=MESH)

    target, has = [], []
    for d in range(6):
        at = [gx, gy, gz]
        if d % 2 == 0:
            has.append(at[d // 2] + 1 < sizes[d // 2])
            at[d // 2] = at[d // 2] + 1
        else:
            has.append(at[d // 2] > 0)
            at[d // 2] = at[d // 2] - 1
        target.append(tuple(at))

    def face_copy(number, source, landing, d, slot):
        return pltpu.make_async_remote_copy(
            src_ref=source,
            dst_ref=landing.at[slot],
            send_sem=face_send.at[number, d],
            recv_sem=face_recv.at[number, slot],
            device_id=target[d],
            device_id_type=MESH,
        )

    def send_face(number, source, landing, d):
        @pl.when(has[d])
        def _():
            face_copy(number, source, landing, d, d ^ 1).start()

    def wait_face(number, source, landing, d):
        @pl.when(has[d])
        def _():
            face_copy(number, source, landing, d, d).wait_recv()

    def wait_sent(number, source, landing, d):
        @pl.when(has[d])
        def _():
            face_copy(number, source, landing, d, d ^ 1).wait_send()

    def reduce_start(number, buf, count, me, peer, send, recv):
        for step in range(1, count):
            pltpu.make_async_remote_copy(
                src_ref=buf.at[number, me],
                dst_ref=buf.at[number, me],
                send_sem=send.at[number, step - 1],
                recv_sem=recv.at[number, step - 1],
                device_id=peer(step),
                device_id_type=MESH,
            ).start()

    def reduce_wait(number, buf, count, me, peer, send, recv, sent):
        for step in range(1, count):
            came = me if sent else lax.rem(me + count - step, count)
            copy = pltpu.make_async_remote_copy(
                src_ref=buf.at[number, me],
                dst_ref=buf.at[number, came],
                send_sem=send.at[number, step - 1],
                recv_sem=recv.at[number, step - 1],
                device_id=peer(step),
                device_id_type=MESH,
            )
            if sent:
                copy.wait_send()
            else:
                copy.wait_recv()

    plane_args = (plane_buf, planes, here, plane_peer, plane_send, plane_recv)
    line_args = (line_buf, nx, gx, line_peer, line_send, line_recv)

    def pack(values):
        parts = []
        for value in values:
            row = jnp.sum(value, axis=0, keepdims=True)
            for j in range(cols // LANES):
                parts.append(row[:, j * LANES : (j + 1) * LANES])
        spare = plane_buf.shape[2] - len(parts)
        if spare:
            parts.append(jnp.zeros((spare, LANES), F32))
        return jnp.concatenate(parts, axis=0)

    def unpack(total, i):
        n = cols // LANES
        return jnp.concatenate([total[i * n + j : i * n + j + 1] for j in range(n)], axis=1)

    def total_of(buf, number, count):
        total = buf[number, 0]
        for i in range(1, count):
            total = total + buf[number, i]
        return total

    def folded(x):
        return jnp.sum(x.reshape(x.shape[0] // 8, 8, cols), axis=0)

    for d in range(6):
        @pl.when(jnp.logical_not(has[d]))
        def _(d=d):
            load_recv[d] = jnp.zeros(load_recv.shape[1:], F32)
            prec_recv[d] = jnp.zeros(prec_recv.shape[1:], F32)
            u1_recv[d] = jnp.zeros(u1_recv.shape[1:], F32)
            u2_recv[d] = jnp.zeros(u2_recv.shape[1:], F32)

    order = (2, 3, 0, 1, 4, 5)
    pl.semaphore_wait(barrier, planes - 1 + nx - 1)
    for d in order:
        send_face(0, load_send.at[d], load_recv, d)
    for d in order:
        send_face(1, prec_send.at[d], prec_recv, d)

    square = jnp.zeros((8, cols), F32)
    for d in order:
        wait_face(0, load_send.at[d], load_recv, d)
        value = load_send[d] + load_recv[d]
        rhs[d] = value
        square = square + folded(value * value)

    def precondition(s, value, wide):
        high = value.astype(BF16)
        low = (value - high.astype(F32)).astype(BF16)
        both = prec_split[s]
        z = jnp.dot(both, jnp.concatenate([high, high], axis=0), preferred_element_type=F32)
        z = z + jnp.dot(both[:, :blk], low, preferred_element_type=F32)
        wide[s] = z
        z_narrow[s * blk : (s + 1) * blk] = z.astype(BF16)

    def operate(d, wide):
        product = jnp.dot(
            schur_slots[d * rows : (d + 1) * rows], z_narrow[...], preferred_element_type=F32
        )
        scale = diag_slots[d * rows : (d + 1) * rows]
        scale = jnp.concatenate([scale] * (cols // LANES), axis=1)
        return product + scale * wide[d * cap : (d + 1) * cap].reshape(rows, cols)

    for d in order:
        wait_face(1, prec_send.at[d], prec_recv, d)
        for k in range(cap):
            s = d * cap + k
            block = prec_send[d, k] + prec_recv[d, k]
            high = block.astype(BF16)
            low = (block - high.astype(F32)).astype(BF16)
            prec_split[s] = jnp.concatenate([high, low], axis=1)
            precondition(s, rhs[d, k * blk : (k + 1) * blk], z1_ref)
    cross = jnp.zeros((8, cols), F32)
    for d in order:
        value = operate(d, z1_ref)
        u1_send[d] = value
        cross = cross + folded(value * rhs[d])

    plane_buf[0, here] = pack((0.5 * square, cross))
    reduce_start(0, *plane_args)
    for d in (2, 3, 4, 5):
        send_face(2, u1_send.at[d], u1_recv, d)
    reduce_wait(0, *plane_args, False)
    line_buf[0, gx] = total_of(plane_buf, 0, planes)
    reduce_start(0, *line_args)
    for d in (0, 1):
        send_face(2, u1_send.at[d], u1_recv, d)
    reduce_wait(0, *line_args, False)
    total = total_of(line_buf, 0, nx)
    load_square = unpack(total, 0)
    beta_square = load_square + EPS
    beta = jnp.sqrt(beta_square)
    h11 = unpack(total, 1) / beta_square

    square = jnp.zeros((8, cols), F32)
    for d in (4, 5, 0, 1, 2, 3):
        wait_face(2, u1_send.at[d], u1_recv, d)
        for k in range(cap):
            s = d * cap + k
            part = slice(k * blk, (k + 1) * blk)
            w = (u1_send[d, part] + u1_recv[d, part]) * mask_ref[s, 0:1]
            value = w - h11 * rhs[d, part]
            q_ref[d, part] = value
            square = square + folded(value * value)
            precondition(s, value, z2_ref)
    first = jnp.zeros((8, cols), F32)
    second = jnp.zeros((8, cols), F32)
    half = rows // 2

    def part_sent(d):
        return u2_send.at[d, pl.ds(half if d % 2 == 0 else 0, half)]

    for d in order:
        value = operate(d, z2_ref)
        u2_send[d] = value
        first = first + folded(value * rhs[d])
        second = second + folded(value * q_ref[d])
    for d in order:
        send_face(3, part_sent(d), u2_recv, d)
    work = jnp.zeros((8, cols), F32)
    step_rows = min(half, blk)
    for d in (4, 5, 0, 1, 2, 3):
        wait_face(3, part_sent(d), u2_recv, d)
        begin = 0 if d % 2 == 0 else half
        for row in range(0, half, step_rows):
            s = d * cap + (begin + row) // blk
            w = u2_send[d, begin + row : begin + row + step_rows]
            w = (w + u2_recv[d, row : row + step_rows]) * mask_ref[s, 0:1]
            work = work + folded(w * w)

    plane_buf[1, here] = pack((0.5 * square, first, second, work))
    reduce_start(1, *plane_args)
    reduce_wait(1, *plane_args, False)
    line_buf[1, gx] = total_of(plane_buf, 1, planes)
    reduce_start(1, *line_args)
    reduce_wait(1, *line_args, False)
    total = total_of(line_buf, 1, nx)
    q_square = unpack(total, 0)
    inverse = 1.0 / beta
    h21 = jnp.sqrt(q_square * inverse * inverse + EPS)
    t = inverse / h21
    h12 = unpack(total, 1) * t * inverse
    a22 = unpack(total, 2) * t * t
    ww = unpack(total, 3) * t * t
    n1 = load_square * inverse * inverse
    n2 = q_square * t * t
    g12 = h11 * EPS * inverse * t
    h22 = a22 - h12 * g12
    left = (
        ww
        - h12 * h12 * (2.0 - n1)
        - h22 * (2.0 * a22 - h22 * n2)
        + 2.0 * h12 * h22 * g12
    )
    h32 = jnp.sqrt(jnp.maximum(left, 0.0) + EPS)
    r1 = jnp.sqrt(h11 * h11 + h21 * h21)
    c1 = h11 / r1
    s1 = h21 / r1
    top = c1 * h12 + s1 * h22
    low = c1 * h22 - s1 * h12
    r2 = jnp.sqrt(low * low + h32 * h32)
    c2 = low / r2
    s2 = h32 / r2
    y2 = -beta * s1 * c2 / r2
    y1 = (beta * c1 - top * y2) / r1
    norm_ref[...] = beta * s1 * s2
    weight1 = y1 * inverse
    weight2 = y2 * t
    for k in range(slots):
        out_ref[k] = weight1 * z1_ref[k] + weight2 * z2_ref[k]

    for d in range(6):
        wait_sent(0, load_send.at[d], load_recv, d)
        wait_sent(1, prec_send.at[d], prec_recv, d)
        wait_sent(2, u1_send.at[d], u1_recv, d)
        wait_sent(3, part_sent(d), u2_recv, d)
    for number in range(2):
        reduce_wait(number, *plane_args, True)
        reduce_wait(number, *line_args, True)


def gather(table, schur_hbm, diag_ref, precond, load, load_out, prec_out, schur_out, diag_out, mask_out, strips, sems):
    nblk, blk, _ = precond.shape
    cols = load.shape[-1]
    slots = table.shape[0]
    cap = slots // 6
    index = [jnp.minimum(table[s], nblk - 1) for s in range(slots)]
    copies = []
    for s in range(slots):
        at = pl.ds(pl.multiple_of(index[s] * blk, blk), blk)
        copies.append(pltpu.make_async_copy(schur_hbm.at[at], strips.at[s], sems.at[s]))
        copies[-1].start()
    eye = lax.broadcasted_iota(jnp.int32, (blk, blk), 0) == lax.broadcasted_iota(
        jnp.int32, (blk, blk), 1
    )
    for s in range(slots):
        d, k = divmod(s, cap)
        valid = table[s] < nblk
        load_out[d, k * blk : (k + 1) * blk] = jnp.where(valid, load[index[s]].astype(F32), 0.0)
        prec_out[d, k] = precond[index[s]]
        mask_out[s] = jnp.full((8, cols), jnp.where(valid, 1.0, 0.0), F32)
        line = diag_ref[:, pl.ds(pl.multiple_of(index[s] * blk, blk), blk)]
        column = jnp.sum(jnp.where(eye, line, 0.0), axis=1, keepdims=True)
        diag_out[s * blk : (s + 1) * blk] = jnp.broadcast_to(column, (blk, LANES))
    for s in range(slots):
        copies[s].wait()
        for t in range(slots):
            at = pl.ds(pl.multiple_of(index[t] * blk, blk), blk)
            schur_out[s * blk : (s + 1) * blk, t * blk : (t + 1) * blk] = strips[s, :, at]


def place(table, compact, out_ref):
    slots = table.shape[0]
    many = out_ref.shape[0]
    first = pl.program_id(0) * many
    for b in range(many):
        found = jnp.int32(slots)
        for s in range(slots):
            found = jnp.where(table[s] == first + b, jnp.int32(s), found)
        value = compact[jnp.minimum(found, slots - 1)]
        out_ref[b] = jnp.where(found < slots, value, 0.0)


def on_device(sizes, schur, interface_diag, precond, load, face_blocks):
    nblk, blk = precond.shape[3:5]
    cols = load.shape[-1]
    order = schur.shape[-1]
    cap = face_blocks.shape[-1]
    slots = 6 * cap
    rows = cap * blk
    nx, ny, nz = sizes
    planes = ny * nz
    packed = -(-(4 * cols // LANES) // 8) * 8
    vmem = pltpu.VMEM
    dma = pltpu.SemaphoreType.DMA
    anywhere = pl.BlockSpec(memory_space=pl.ANY)
    local = pl.BlockSpec(memory_space=pltpu.VMEM)
    scalars = pl.BlockSpec(memory_space=pltpu.SMEM)
    table = face_blocks.reshape(slots)
    mib = 1024 * 1024
    gathered = pl.pallas_call(
        gather,
        out_shape=(
            jax.ShapeDtypeStruct((6, rows, cols), F32),
            jax.ShapeDtypeStruct((6, cap, blk, blk), F32),
            jax.ShapeDtypeStruct((slots * blk, slots * blk), BF16),
            jax.ShapeDtypeStruct((slots * blk, LANES), F32),
            jax.ShapeDtypeStruct((slots, 8, cols), F32),
        ),
        in_specs=[scalars, anywhere, local, local, local],
        out_specs=(local,) * 5,
        scratch_shapes=[vmem((slots, blk, order), BF16), dma((slots,))],
        compiler_params=pltpu.CompilerParams(vmem_limit_bytes=24 * mib),
    )(
        table,
        schur.reshape(order, order),
        interface_diag.reshape(1, order),
        precond.reshape(nblk, blk, blk),
        load.reshape(nblk, blk, cols),
    )
    compact, norm = pl.pallas_call(
        functools.partial(kernel, sizes),
        out_shape=(
            jax.ShapeDtypeStruct((slots, blk, cols), F32),
            jax.ShapeDtypeStruct((1, cols), F32),
        ),
        in_specs=[local] * 5,
        out_specs=(local, local),
        scratch_shapes=[
            vmem((6, rows, cols), F32),
            vmem((6, cap, blk, blk), F32),
            vmem((slots, blk, 2 * blk), BF16),
            vmem((6, rows, cols), F32),
            vmem((slots, blk, cols), F32),
            vmem((slots, blk, cols), F32),
            vmem((slots * blk, cols), BF16),
            vmem((6, rows, cols), F32),
            vmem((6, rows, cols), F32),
            vmem((6, rows, cols), F32),
            vmem((6, rows, cols), F32),
            vmem((6, rows // 2, cols), F32),
            vmem((2, planes, packed, LANES), F32),
            vmem((2, nx, packed, LANES), F32),
            dma((4, 6)),
            dma((4, 6)),
            dma((2, max(planes - 1, 1))),
            dma((2, max(planes - 1, 1))),
            dma((2, max(nx - 1, 1))),
            dma((2, max(nx - 1, 1))),
        ],
        compiler_params=pltpu.CompilerParams(
            collective_id=0, has_side_effects=True, vmem_limit_bytes=32 * mib
        ),
    )(*gathered)
    many = 4 if nblk % 4 == 0 else 1
    result = pl.pallas_call(
        place,
        grid=(nblk // many,),
        out_shape=jax.ShapeDtypeStruct((nblk, blk, cols), F32),
        in_specs=[scalars, local],
        out_specs=pl.BlockSpec((many, blk, cols), lambda i: (i, 0, 0)),
        compiler_params=pltpu.CompilerParams(vmem_limit_bytes=16 * mib),
    )(table, compact)
    return result.reshape(1, 1, 1, nblk * blk, cols), norm.reshape(cols)


def solution(mesh):
    sizes = tuple(mesh.shape[a] for a in AXES)
    placed = (
        P("gx", "gy", "gz", None, None),
        P("gx", "gy", "gz", None),
        P("gx", "gy", "gz", None, None, None),
        P("gx", "gy", "gz", None, None),
        P("gx", "gy", "gz", None, None),
    )
    return jax.shard_map(
        functools.partial(on_device, sizes),
        mesh=mesh,
        in_specs=placed,
        out_specs=(P("gx", "gy", "gz", None, None), P()),
        check_vma=False,
    )
```

time: 335 us -> 69.3 us (0.21)
  blocking collectives: 85.7 us -> 0 us
  starting transfers between devices: 78.9 us -> 0 us
  local copies, waits for them, and re-layouts: 83.5 us -> 7.94 us
  Pallas kernels: 0 us -> 60.4 us
  other arithmetic: 39.8 us -> 0 us
  matrix products: 25.2 us -> 0 us
  waiting for transfers between devices: 18.6 us -> 0 us
    psum x2 -> x0, blocking collectives: 85.7 us -> none  [the longest x1 43.7 us: on_device(): lax.psum((partial_product(assembled_load, assembled_load), partial_produc...]
    ppermute x30 -> x0, starting transfers between devices: 78.9 us -> none  [the longest x15 59.6 us: extended_2(): before = lax.ppermute(last, axis, up)]
    pallas_call x0 -> x3, Pallas kernels: none -> 60.4 us  [the longest x1 55.2 us: on_device(): pl.pallas_call(functools.partial(kernel, sizes), out_shape=(jax.ShapeDtyp...]
    dot_general x4 -> x0, matrix products: 25.2 us -> none  [the longest x2 15.7 us: operate(): product = jnp.dot(matrix, narrow, preferred_element_type=jnp.float32)]
    scatter-add x5 -> x0, other arithmetic: 21.2 us -> none  [assemble(): extended.at[slot_flat]]
    ppermute x30 -> x0, waiting for transfers between devices: 18.6 us -> none  [the longest x15 13.1 us: extended_2(): before = lax.ppermute(last, axis, up)]
    concatenate x6 -> x0, local copies, waits for them, and re-layouts: 15.7 us -> none  [assemble(): jnp.concatenate([blocks, jnp.zeros((1, block_rows, row_width), jnp.float3...]
    gather x5 -> x0, local copies, waits for them, and re-layouts: 15.5 us -> none  [assemble(): packed = extended[slot_flat].reshape(6, slot_count, block_rows, row_width)]
  transfers between devices with their start and end apart: 30 -> 0, of which waited for: 9 -> 0; matrix products, arithmetic and copies ran while one was open for 8% -> 0% of each run, Pallas kernels for 0% -> 0%
where the time goes in v1:
time: 69.3 us; the launch traced here: 69 us
  Pallas kernels  60.4 us (87%)
  local copies, waits for them, and re-layouts  7.94 us (11%)
    pallas_call x1, Pallas kernels, on_device(): pl.pallas_call(functools.partial(kernel, sizes), out_shape=(jax.ShapeDtyp...  55.2 us
    unnamed x10, local copies, waits for them, and re-layouts  7.86 us
    pallas_call x1, Pallas kernels, on_device(): pl.pallas_call(gather, out_shape=(jax.ShapeDtypeStruct((6, rows, cols), F...  2.72 us
    pallas_call x1, Pallas kernels, on_device(): pl.pallas_call(place, grid=(nblk // many,), out_shape=jax.ShapeDtypeStruc...  2.5 us

profile of v1, /device:TPU:0, one launch (start us, length us, event | category | flops | bytes accessed | tf_op | source)
XLA Modules:
  0.0 69.0 jit_solution(9260395753703426851)
XLA Ops:
  0.6 0.8 %copy.8 = s32[1,1,1,6,2]{4,3,2,1,0:T(8,128)S(1)} copy(s32[1,1,1,6,2]{3,4,2,1,0:T(2,128)} %param.9) | data formatting | bytes 96 | tf_op args[4]
  1.4 0.1 reshape.25.table
  1.5 0.0 copy-start
  1.5 3.4 %copy-done = bf16[1,1,1,2048,2048]{4,3,2,1,0:T(8,128)(2,1)S(1)} copy-done((bf16[1,1,1,2048,2048]{4,3,2,1,0:T(8,128)(2,1)S(1)}, bf16[1,1,1,2048,2048]{4,3,2,1,0:T(8,128)(2,1)}, u32[]{:S(2)}) %copy-start) | copy-done | bytes 8388632
  4.9 0.0 copy-start.1
  4.9 1.2 %copy-done.1 = f32[1,1,1,16,128,128]{5,4,3,2,1,0:T(8,128)S(1)} copy-done((f32[1,1,1,16,128,128]{5,4,3,2,1,0:T(8,128)S(1)}, f32[1,1,1,16,128,128]{5,4,3,2,1,0:T(8,128)}, u32[]{:S(2)}) %copy-start.1) | copy-done | bytes 1048600
  6.1 0.0 copy-start.2
  6.1 1.2 %copy-done.2 = bf16[1,1,1,2048,256]{4,3,2,1,0:T(8,128)(2,1)S(1)} copy-done((bf16[1,1,1,2048,256]{4,3,2,1,0:T(8,128)(2,1)S(1)}, bf16[1,1,1,2048,256]{4,3,2,1,0:T(8,128)(2,1)}, u32[]{:S(2)}) %copy-start.2) | copy-done | bytes 1048600
  7.3 0.0 copy-start.3
  7.3 0.7 %copy-done.3 = f32[1,1,1,2048]{3,2,1,0:T(1,128)S(1)} copy-done((f32[1,1,1,2048]{3,2,1,0:T(1,128)S(1)}, f32[1,1,1,2048]{3,2,1,0:T(1,128)}, u32[]{:S(2)}) %copy-start.3) | copy-done | bytes 8216
  8.0 2.7 %shard_map.68 = (f32[6,256,256]{2,1,0:T(8,128)S(1)}, f32[6,2,128,128]{3,2,1,0:T(8,128)S(1)}, bf16[1536,1536]{1,0:T(8,128)(2,1)S(1)}, f32[1536,128]{1,0:T(8,128)S(1)}, f32[12,8,256]{2,1,0:T(8,128)S(1)}) custom-call(s32[12]{0:T(128)S(1)} %reshape.25.table, bf16[2048,2048]{1,0:T(8,128)(2,1)S(1)} %bitcast.6, f32[1,2048]{1,0:T(1,128)S(1)} %bitcast.9, ...), custom_call_target="tpu_custom_call" | custom-call | tf_op jit(solution)/shard_map/pallas_call | solution.py:376
  10.7 55.2 %shard_map.69 = (f32[12,128,256]{2,1,0:T(8,128)S(1)}, f32[1,256]{1,0:T(1,128)S(1)}) custom-call(f32[6,256,256]{2,1,0:T(8,128)S(1)} %get-tuple-element.9.load_send, f32[6,2,128,128]{3,2,1,0:T(8,128)S(1)} %get-tuple-element.10.prec_send, bf16[1536,1536]{1,0:T(8,128)(2,1)S(1)} %get-tuple-element.11.schur_slots, f32[1536,128]{1,0:T(8,128)S(1)} %get-tuple-element.12.diag_slots, ...), custom_call_target="tpu_custom_call" | custom-call | tf_op jit(solution)/shard_map/pallas_call | solution.py:396
  65.9 2.5 %shard_map.70 = f32[16,128,256]{2,1,0:T(8,128)} custom-call(s32[12]{0:T(128)S(1)} %reshape.25.table, f32[12,128,256]{2,1,0:T(8,128)S(1)} %get-tuple-element.14.compact), custom_call_target="tpu_custom_call" | custom-call | tf_op jit(solution)/shard_map/pallas_call | solution.py:431
  68.4 0.6 copy.10
Async XLA Ops:
  1.5 3.4 %copy-start = (bf16[1,1,1,2048,2048]{4,3,2,1,0:T(8,128)(2,1)S(1)}, bf16[1,1,1,2048,2048]{4,3,2,1,0:T(8,128)(2,1)}, u32[]{:S(2)}) copy-start(bf16[1,1,1,2048,2048]{4,3,2,1,0:T(8,128)(2,1)} %param.5) | copy-start | bytes 25165828
  4.9 1.2 %copy-start.1 = (f32[1,1,1,16,128,128]{5,4,3,2,1,0:T(8,128)S(1)}, f32[1,1,1,16,128,128]{5,4,3,2,1,0:T(8,128)}, u32[]{:S(2)}) copy-start(f32[1,1,1,16,128,128]{5,4,3,2,1,0:T(8,128)} %param.7) | copy-start | bytes 3145732
  6.1 1.2 %copy-start.2 = (bf16[1,1,1,2048,256]{4,3,2,1,0:T(8,128)(2,1)S(1)}, bf16[1,1,1,2048,256]{4,3,2,1,0:T(8,128)(2,1)}, u32[]{:S(2)}) copy-start(bf16[1,1,1,2048,256]{4,3,2,1,0:T(8,128)(2,1)} %param.8) | copy-start | bytes 3145732
  7.3 0.7 %copy-start.3 = (f32[1,1,1,2048]{3,2,1,0:T(1,128)S(1)}, f32[1,1,1,2048]{3,2,1,0:T(1,128)}, u32[]{:S(2)}) copy-start(f32[1,1,1,2048]{3,2,1,0:T(1,128)} %param.6) | copy-start | bytes 24580

commit v2 on v1

--- a/solution.py
+++ b/solution.py
@@ -245,13 +245,14 @@
     def part_sent(d):
         return u2_send.at[d, pl.ds(half if d % 2 == 0 else 0, half)]
 
-    for d in order:
+    for i, d in enumerate(order):
         value = operate(d, z2_ref)
         u2_send[d] = value
         first = first + folded(value * rhs[d])
         second = second + folded(value * q_ref[d])
-    for d in order:
-        send_face(3, part_sent(d), u2_recv, d)
+        if i:
+            send_face(3, part_sent(order[i - 1]), u2_recv, order[i - 1])
+    send_face(3, part_sent(order[-1]), u2_recv, order[-1])
     work = jnp.zeros((8, cols), F32)
     step_rows = min(half, blk)
     for d in (4, 5, 0, 1, 2, 3):

time: 69.3 us -> 68.3 us (0.986)
  Pallas kernels: 60.4 us -> 59.5 us
    pallas_call x1, Pallas kernels: 55.2 us -> 54.2 us  [on_device(): pl.pallas_call(functools.partial(kernel, sizes), out_shape=(jax.ShapeDtyp...]
where the time goes in v2:
time: 68.3 us; the launch traced here: 68 us
  Pallas kernels  59.5 us (87%)
  local copies, waits for them, and re-layouts  7.94 us (12%)
    pallas_call x1, Pallas kernels, on_device(): pl.pallas_call(functools.partial(kernel, sizes), out_shape=(jax.ShapeDtyp...  54.2 us
    unnamed x10, local copies, waits for them, and re-layouts  7.86 us
    pallas_call x1, Pallas kernels, on_device(): pl.pallas_call(gather, out_shape=(jax.ShapeDtypeStruct((6, rows, cols), F...  2.72 us
    pallas_call x1, Pallas kernels, on_device(): pl.pallas_call(place, grid=(nblk // many,), out_shape=jax.ShapeDtypeStruc...  2.5 us

profile of v2, /device:TPU:0, one launch (start us, length us, event | category | flops | bytes accessed | tf_op | source)
XLA Modules:
  0.0 68.0 jit_solution(13237446411124929941)
XLA Ops:
  0.6 0.8 %copy.8 = s32[1,1,1,6,2]{4,3,2,1,0:T(8,128)S(1)} copy(s32[1,1,1,6,2]{3,4,2,1,0:T(2,128)} %param.9) | data formatting | bytes 96 | tf_op args[4]
  1.4 0.1 reshape.25.table
  1.5 0.0 copy-start
  1.5 3.4 %copy-done = bf16[1,1,1,2048,2048]{4,3,2,1,0:T(8,128)(2,1)S(1)} copy-done((bf16[1,1,1,2048,2048]{4,3,2,1,0:T(8,128)(2,1)S(1)}, bf16[1,1,1,2048,2048]{4,3,2,1,0:T(8,128)(2,1)}, u32[]{:S(2)}) %copy-start) | copy-done | bytes 8388632
  4.9 0.0 copy-start.1
  4.9 1.2 %copy-done.1 = f32[1,1,1,16,128,128]{5,4,3,2,1,0:T(8,128)S(1)} copy-done((f32[1,1,1,16,128,128]{5,4,3,2,1,0:T(8,128)S(1)}, f32[1,1,1,16,128,128]{5,4,3,2,1,0:T(8,128)}, u32[]{:S(2)}) %copy-start.1) | copy-done | bytes 1048600
  6.1 0.0 copy-start.2
  6.1 1.2 %copy-done.2 = bf16[1,1,1,2048,256]{4,3,2,1,0:T(8,128)(2,1)S(1)} copy-done((bf16[1,1,1,2048,256]{4,3,2,1,0:T(8,128)(2,1)S(1)}, bf16[1,1,1,2048,256]{4,3,2,1,0:T(8,128)(2,1)}, u32[]{:S(2)}) %copy-start.2) | copy-done | bytes 1048600
  7.3 0.0 copy-start.3
  7.3 0.7 %copy-done.3 = f32[1,1,1,2048]{3,2,1,0:T(1,128)S(1)} copy-done((f32[1,1,1,2048]{3,2,1,0:T(1,128)S(1)}, f32[1,1,1,2048]{3,2,1,0:T(1,128)}, u32[]{:S(2)}) %copy-start.3) | copy-done | bytes 8216
  8.0 2.7 %shard_map.68 = (f32[6,256,256]{2,1,0:T(8,128)S(1)}, f32[6,2,128,128]{3,2,1,0:T(8,128)S(1)}, bf16[1536,1536]{1,0:T(8,128)(2,1)S(1)}, f32[1536,128]{1,0:T(8,128)S(1)}, f32[12,8,256]{2,1,0:T(8,128)S(1)}) custom-call(s32[12]{0:T(128)S(1)} %reshape.25.table, bf16[2048,2048]{1,0:T(8,128)(2,1)S(1)} %bitcast.6, f32[1,2048]{1,0:T(1,128)S(1)} %bitcast.9, ...), custom_call_target="tpu_custom_call" | custom-call | tf_op jit(solution)/shard_map/pallas_call | solution.py:377
  10.7 54.2 %shard_map.69 = (f32[12,128,256]{2,1,0:T(8,128)S(1)}, f32[1,256]{1,0:T(1,128)S(1)}) custom-call(f32[6,256,256]{2,1,0:T(8,128)S(1)} %get-tuple-element.9.load_send, f32[6,2,128,128]{3,2,1,0:T(8,128)S(1)} %get-tuple-element.10.prec_send, bf16[1536,1536]{1,0:T(8,128)(2,1)S(1)} %get-tuple-element.11.schur_slots, f32[1536,128]{1,0:T(8,128)S(1)} %get-tuple-element.12.diag_slots, ...), custom_call_target="tpu_custom_call" | custom-call | tf_op jit(solution)/shard_map/pallas_call | solution.py:397
  65.0 2.5 %shard_map.70 = f32[16,128,256]{2,1,0:T(8,128)} custom-call(s32[12]{0:T(128)S(1)} %reshape.25.table, f32[12,128,256]{2,1,0:T(8,128)S(1)} %get-tuple-element.14.compact), custom_call_target="tpu_custom_call" | custom-call | tf_op jit(solution)/shard_map/pallas_call | solution.py:432
  67.5 0.6 copy.10
Async XLA Ops:
  1.5 3.4 %copy-start = (bf16[1,1,1,2048,2048]{4,3,2,1,0:T(8,128)(2,1)S(1)}, bf16[1,1,1,2048,2048]{4,3,2,1,0:T(8,128)(2,1)}, u32[]{:S(2)}) copy-start(bf16[1,1,1,2048,2048]{4,3,2,1,0:T(8,128)(2,1)} %param.5) | copy-start | bytes 25165828
  4.9 1.2 %copy-start.1 = (f32[1,1,1,16,128,128]{5,4,3,2,1,0:T(8,128)S(1)}, f32[1,1,1,16,128,128]{5,4,3,2,1,0:T(8,128)}, u32[]{:S(2)}) copy-start(f32[1,1,1,16,128,128]{5,4,3,2,1,0:T(8,128)} %param.7) | copy-start | bytes 3145732
  6.1 1.2 %copy-start.2 = (bf16[1,1,1,2048,256]{4,3,2,1,0:T(8,128)(2,1)S(1)}, bf16[1,1,1,2048,256]{4,3,2,1,0:T(8,128)(2,1)}, u32[]{:S(2)}) copy-start(bf16[1,1,1,2048,256]{4,3,2,1,0:T(8,128)(2,1)} %param.8) | copy-start | bytes 3145732
  7.3 0.7 %copy-start.3 = (f32[1,1,1,2048]{3,2,1,0:T(1,128)S(1)}, f32[1,1,1,2048]{3,2,1,0:T(1,128)}, u32[]{:S(2)}) copy-start(f32[1,1,1,2048]{3,2,1,0:T(1,128)} %param.6) | copy-start | bytes 24580

commit v3 on v2

--- a/solution.py
+++ b/solution.py
@@ -166,6 +166,7 @@
             u2_recv[d] = jnp.zeros(u2_recv.shape[1:], F32)
 
     order = (2, 3, 0, 1, 4, 5)
+    arrival = (4, 5, 0, 1, 2, 3)
     pl.semaphore_wait(barrier, planes - 1 + nx - 1)
     for d in order:
         send_face(0, load_send.at[d], load_recv, d)
@@ -173,7 +174,7 @@
         send_face(1, prec_send.at[d], prec_recv, d)
 
     square = jnp.zeros((8, cols), F32)
-    for d in order:
+    for d in arrival:
         wait_face(0, load_send.at[d], load_recv, d)
         value = load_send[d] + load_recv[d]
         rhs[d] = value
@@ -196,7 +197,7 @@
         scale = jnp.concatenate([scale] * (cols // LANES), axis=1)
         return product + scale * wide[d * cap : (d + 1) * cap].reshape(rows, cols)
 
-    for d in order:
+    for d in arrival:
         wait_face(1, prec_send.at[d], prec_recv, d)
         for k in range(cap):
             s = d * cap + k
@@ -228,7 +229,7 @@
     h11 = unpack(total, 1) / beta_square
 
     square = jnp.zeros((8, cols), F32)
-    for d in (4, 5, 0, 1, 2, 3):
+    for d in arrival:
         wait_face(2, u1_send.at[d], u1_recv, d)
         for k in range(cap):
             s = d * cap + k
@@ -255,7 +256,7 @@
     send_face(3, part_sent(order[-1]), u2_recv, order[-1])
     work = jnp.zeros((8, cols), F32)
     step_rows = min(half, blk)
-    for d in (4, 5, 0, 1, 2, 3):
+    for d in arrival:
         wait_face(3, part_sent(d), u2_recv, d)
         begin = 0 if d % 2 == 0 else half
         for row in range(0, half, step_rows):

time: 68.3 us -> 67.4 us (0.987)
  Pallas kernels: 59.5 us -> 58.6 us
    pallas_call x1, Pallas kernels: 54.2 us -> 53.3 us  [on_device(): pl.pallas_call(functools.partial(kernel, sizes), out_shape=(jax.ShapeDtyp...]
where the time goes in v3:
time: 67.4 us; the launch traced here: 67.1 us
  Pallas kernels  58.6 us (87%)
  local copies, waits for them, and re-layouts  7.94 us (12%)
    pallas_call x1, Pallas kernels, on_device(): pl.pallas_call(functools.partial(kernel, sizes), out_shape=(jax.ShapeDtyp...  53.3 us
    unnamed x10, local copies, waits for them, and re-layouts  7.86 us
    pallas_call x1, Pallas kernels, on_device(): pl.pallas_call(gather, out_shape=(jax.ShapeDtypeStruct((6, rows, cols), F...  2.72 us
    pallas_call x1, Pallas kernels, on_device(): pl.pallas_call(place, grid=(nblk // many,), out_shape=jax.ShapeDtypeStruc...  2.5 us

profile of v3, /device:TPU:0, one launch (start us, length us, event | category | flops | bytes accessed | tf_op | source)
XLA Modules:
  0.0 67.1 jit_solution(14255348778140802650)
XLA Ops:
  0.6 0.8 %copy.8 = s32[1,1,1,6,2]{4,3,2,1,0:T(8,128)S(1)} copy(s32[1,1,1,6,2]{3,4,2,1,0:T(2,128)} %param.9) | data formatting | bytes 96 | tf_op args[4]
  1.4 0.1 reshape.25.table
  1.5 0.0 copy-start
  1.5 3.4 %copy-done = bf16[1,1,1,2048,2048]{4,3,2,1,0:T(8,128)(2,1)S(1)} copy-done((bf16[1,1,1,2048,2048]{4,3,2,1,0:T(8,128)(2,1)S(1)}, bf16[1,1,1,2048,2048]{4,3,2,1,0:T(8,128)(2,1)}, u32[]{:S(2)}) %copy-start) | copy-done | bytes 8388632
  4.9 0.0 copy-start.1
  4.9 1.2 %copy-done.1 = f32[1,1,1,16,128,128]{5,4,3,2,1,0:T(8,128)S(1)} copy-done((f32[1,1,1,16,128,128]{5,4,3,2,1,0:T(8,128)S(1)}, f32[1,1,1,16,128,128]{5,4,3,2,1,0:T(8,128)}, u32[]{:S(2)}) %copy-start.1) | copy-done | bytes 1048600
  6.1 0.0 copy-start.2
  6.1 1.2 %copy-done.2 = bf16[1,1,1,2048,256]{4,3,2,1,0:T(8,128)(2,1)S(1)} copy-done((bf16[1,1,1,2048,256]{4,3,2,1,0:T(8,128)(2,1)S(1)}, bf16[1,1,1,2048,256]{4,3,2,1,0:T(8,128)(2,1)}, u32[]{:S(2)}) %copy-start.2) | copy-done | bytes 1048600
  7.3 0.0 copy-start.3
  7.3 0.7 %copy-done.3 = f32[1,1,1,2048]{3,2,1,0:T(1,128)S(1)} copy-done((f32[1,1,1,2048]{3,2,1,0:T(1,128)S(1)}, f32[1,1,1,2048]{3,2,1,0:T(1,128)}, u32[]{:S(2)}) %copy-start.3) | copy-done | bytes 8216
  8.0 2.7 %shard_map.68 = (f32[6,256,256]{2,1,0:T(8,128)S(1)}, f32[6,2,128,128]{3,2,1,0:T(8,128)S(1)}, bf16[1536,1536]{1,0:T(8,128)(2,1)S(1)}, f32[1536,128]{1,0:T(8,128)S(1)}, f32[12,8,256]{2,1,0:T(8,128)S(1)}) custom-call(s32[12]{0:T(128)S(1)} %reshape.25.table, bf16[2048,2048]{1,0:T(8,128)(2,1)S(1)} %bitcast.6, f32[1,2048]{1,0:T(1,128)S(1)} %bitcast.9, ...), custom_call_target="tpu_custom_call" | custom-call | tf_op jit(solution)/shard_map/pallas_call | solution.py:378
  10.7 53.3 %shard_map.69 = (f32[12,128,256]{2,1,0:T(8,128)S(1)}, f32[1,256]{1,0:T(1,128)S(1)}) custom-call(f32[6,256,256]{2,1,0:T(8,128)S(1)} %get-tuple-element.9.load_send, f32[6,2,128,128]{3,2,1,0:T(8,128)S(1)} %get-tuple-element.10.prec_send, bf16[1536,1536]{1,0:T(8,128)(2,1)S(1)} %get-tuple-element.11.schur_slots, f32[1536,128]{1,0:T(8,128)S(1)} %get-tuple-element.12.diag_slots, ...), custom_call_target="tpu_custom_call" | custom-call | tf_op jit(solution)/shard_map/pallas_call | solution.py:398
  64.1 2.5 %shard_map.70 = f32[16,128,256]{2,1,0:T(8,128)} custom-call(s32[12]{0:T(128)S(1)} %reshape.25.table, f32[12,128,256]{2,1,0:T(8,128)S(1)} %get-tuple-element.14.compact), custom_call_target="tpu_custom_call" | custom-call | tf_op jit(solution)/shard_map/pallas_call | solution.py:433
  66.6 0.6 copy.10
Async XLA Ops:
  1.5 3.4 %copy-start = (bf16[1,1,1,2048,2048]{4,3,2,1,0:T(8,128)(2,1)S(1)}, bf16[1,1,1,2048,2048]{4,3,2,1,0:T(8,128)(2,1)}, u32[]{:S(2)}) copy-start(bf16[1,1,1,2048,2048]{4,3,2,1,0:T(8,128)(2,1)} %param.5) | copy-start | bytes 25165828
  4.9 1.2 %copy-start.1 = (f32[1,1,1,16,128,128]{5,4,3,2,1,0:T(8,128)S(1)}, f32[1,1,1,16,128,128]{5,4,3,2,1,0:T(8,128)}, u32[]{:S(2)}) copy-start(f32[1,1,1,16,128,128]{5,4,3,2,1,0:T(8,128)} %param.7) | copy-start | bytes 3145732
  6.1 1.2 %copy-start.2 = (bf16[1,1,1,2048,256]{4,3,2,1,0:T(8,128)(2,1)S(1)}, bf16[1,1,1,2048,256]{4,3,2,1,0:T(8,128)(2,1)}, u32[]{:S(2)}) copy-start(bf16[1,1,1,2048,256]{4,3,2,1,0:T(8,128)(2,1)} %param.8) | copy-start | bytes 3145732
  7.3 0.7 %copy-start.3 = (f32[1,1,1,2048]{3,2,1,0:T(1,128)S(1)}, f32[1,1,1,2048]{3,2,1,0:T(1,128)}, u32[]{:S(2)}) copy-start(f32[1,1,1,2048]{3,2,1,0:T(1,128)} %param.6) | copy-start | bytes 24580
